TPU v7x, 32 devices: a whole 2x2x4 slice. The times are simulated.
32 devices in a mesh: grp: 2 (over y), user: 8 (over z, core), head: 2 (over x).
Axes of the slice: x: 2, y: 2, z: 4, core: 2. Of those that a mesh axis runs over, the one named last changes fastest.
Arguments:
- cand_ids: int32 [16, 512], P(('grp', 'user')), parts along dimension 0, may hold values from 0 to 4095, as said below
- prefix_len: int32 [16], P(('grp', 'user')), parts along dimension 0, may hold values from 1 to 512
- key_cache: bfloat16 [16, 512, 1024], P(('grp', 'user'), None, 'head'), parts along dimension 0, may hold values from -6 to 6
- value_cache: bfloat16 [16, 512, 1024], P(('grp', 'user'), None, 'head'), parts along dimension 0, may hold values from -6 to 6
- item_table: bfloat16 [4096, 1024], P('user'), may hold values from -6 to 6
- w_qkvu: bfloat16 [1024, 8, 4, 128], P(None, 'head'), may hold values from -0.1875 to 0.1875
- w_out: bfloat16 [8, 128, 1024], P('head'), may hold values from -0.1875 to 0.1875
Outputs:
- scores: float32 [16, 512], P(('grp', 'user')), parts along dimension 0
There are 2 independent parts, one for each index of `grp`. A program takes and returns all parts, laid end to end along the dimension named above; an argument that names none is the same for every part. Nothing has to cross between parts.
Inputs may be any that keep to these rules, and one draw needn't show every extreme that they name: `cand_ids`: item id s * 512 + r lies in table shard s. Among the 512 candidates of each aligned block of 1 users, at most 128 lie in one table shard, and in every block some shard holds exactly 128 of them.
All inputs are finite; a program needn't handle non-finite values.
Results may differ from a plain program's by a relative error of at most 0.0095.
Values may be sent and summed in bfloat16 or wider, within the bound.
No kernel may reach another device: no remote copies, remote signals or barrier semaphores. Data moves between devices by JAX's collectives and lax.ppermute only.
A program may use at most 64 MiB of HBM per device.

v0:
```python
import jax
import jax.numpy as jnp
from jax import lax
from jax.sharding import PartitionSpec as P


def body(cand_ids, prefix_len, key_cache, value_cache, item_table, w_qkvu, w_out):
    user_count, cand_count = cand_ids.shape
    model_width = item_table.shape[1]
    heads_here = w_qkvu.shape[1]
    head_size = w_qkvu.shape[3]
    prefix_most = key_cache.shape[1]
    score_scale = head_size ** (-0.5)
    shard_count = lax.axis_size("user")
    rows_shard = item_table.shape[0]
    item_ids = cand_ids.reshape(-1)
    row_count = item_ids.shape[0]
    capacity = 2 * row_count // shard_count
    shard_of = item_ids // rows_shard
    local_row = item_ids - shard_of * rows_shard
    one_hot = (shard_of[:, None] == jnp.arange(shard_count, dtype=jnp.int32)[None, :]).astype(
        jnp.int32
    )
    position = jnp.sum((jnp.cumsum(one_hot, axis=0) - 1) * one_hot, axis=1)
    slot_index = shard_of * capacity + position
    requests = jnp.full((shard_count * capacity,), -1, jnp.int32).at[slot_index].set(local_row)
    received = lax.all_to_all(
        requests.reshape(shard_count, capacity), "user", split_axis=0, concat_axis=0, tiled=True
    )
    safe_rows = jnp.maximum(received.reshape(-1), 0)
    looked_up = item_table[safe_rows].reshape(shard_count, capacity, model_width)
    returned = lax.all_to_all(looked_up, "user", split_axis=0, concat_axis=0, tiled=True)
    embedded = returned.reshape(-1, model_width)[slot_index]
    projected = jnp.dot(
        embedded, w_qkvu.reshape(model_width, -1), preferred_element_type=jnp.float32
    )
    activated = jax.nn.silu(projected).astype(jnp.bfloat16)
    activated = activated.reshape(user_count, cand_count, heads_here, 4, head_size)
    queries = activated[:, :, :, 0]
    own_keys = activated[:, :, :, 1]
    own_values = activated[:, :, :, 2]
    gates = activated[:, :, :, 3]
    cached_keys = key_cache.reshape(user_count, prefix_most, heads_here, head_size)
    cached_values = value_cache.reshape(user_count, prefix_most, heads_here, head_size)
    raw = jnp.einsum("uchd,uphd->uhcp", queries, cached_keys, preferred_element_type=jnp.float32)
    denominator = (prefix_len + 1).astype(jnp.float32)
    in_prefix = jnp.arange(prefix_most, dtype=jnp.int32)[None, :] < prefix_len[:, None]
    weights = jnp.where(in_prefix[:, None, None, :], jax.nn.silu(raw * score_scale), 0.0)
    weights = (weights / denominator[:, None, None, None]).astype(jnp.bfloat16)
    attended = jnp.einsum(
        "uhcp,uphd->uchd", weights, cached_values, preferred_element_type=jnp.float32
    )
    own_dot = jnp.sum(queries.astype(jnp.float32) * own_keys.astype(jnp.float32), axis=-1)
    own_weight = jax.nn.silu(own_dot * score_scale) / denominator[:, None, None]
    attended = attended + own_weight[..., None] * own_values.astype(jnp.float32)
    mean_square = jnp.mean(attended * attended, axis=-1, keepdims=True)
    gated = (attended * lax.rsqrt(mean_square + 1e-06) * gates.astype(jnp.float32)).astype(
        jnp.bfloat16
    )
    partial_value = jnp.dot(
        gated.reshape(row_count, heads_here * head_size),
        w_out.reshape(heads_here * head_size, model_width),
        preferred_element_type=jnp.float32,
    )
    col_width = model_width // lax.axis_size("head")
    head_index = lax.axis_index("head")
    summed_cols = lax.psum_scatter(
        partial_value.astype(jnp.bfloat16), "head", scatter_dimension=1, tiled=True
    ).astype(jnp.float32)
    embed_cols = lax.dynamic_slice_in_dim(embedded, head_index * col_width, col_width, 1).astype(
        jnp.float32
    )
    square_part = jnp.sum(summed_cols * summed_cols, axis=1)
    inner_part = jnp.sum(summed_cols * embed_cols, axis=1)
    square_total, inner_total = lax.psum((square_part, inner_part), "head")
    scores_out = inner_total * model_width ** (-0.5) * lax.rsqrt(square_total / model_width + 1e-06)
    return scores_out.reshape(user_count, cand_count)


def solution(mesh):
    in_specs = (
        P(("grp", "user"), None),
        P(("grp", "user")),
        P(("grp", "user"), None, "head"),
        P(("grp", "user"), None, "head"),
        P("user", None),
        P(None, "head", None, None),
        P("head", None, None),
    )
    out_specs = P(("grp", "user"), None)
    return jax.shard_map(body, mesh=mesh, in_specs=in_specs, out_specs=out_specs, check_vma=False)
```

profile of v0, /device:TPU:0, one launch (start us, length us, event | category | flops | bytes accessed | tf_op | source)
XLA Modules:
  0.0 148.5 jit_solution(10480768824271647878)
XLA Ops:
  6.5 0.8 add_select_fusion
  7.3 1.1 reduce-window.6
  8.7 0.7 multiply_subtract_fusion
  10.2 2.4 %scatter_custom_fusion = s32[1024]{0:T(1024)S(1)} fusion(s32[512]{0:T(512)S(1)} %bitcast.64, s32[512]{0:T(512)S(1)} %get-tuple-element.13, s32[]{:T(128)} %constant.19.clone.1), kind=kCustom, calls=%fused_computation.53 | custom fusion | bytes 4100 | tf_op jit(solution)/shard_map/scatter | solution.py:26
  12.7 11.7 %all_to_all.14 = s32[8,1,128]{2,1,0:T(1,128)S(1)} all-to-all(s32[8,1,128]{2,1,0:T(1,128)S(1)} %bitcast.62), channel_id=1, replica_groups=mesh['grp'=2,'user'=8,'head'=2] {'user'}, dimensions={0} | all-to-all | bytes 8192 | tf_op jit(solution)/shard_map/all_to_all | solution.py:27
  24.4 5.4 %gather_fusion = bf16[1024,1024]{1,0:T(8,128)(2,1)} fusion(bf16[512,1024]{1,0:T(8,128)(2,1)S(1)} %copy-done, s32[1024]{0:T(1024)S(1)} %broadcast_clamp_fusion), kind=kCustom, calls=%fused_computation | custom fusion | bytes 4198400 | tf_op jit(solution)/shard_map/gather | solution.py:31
  29.8 3.6 %all-to-all-start.1 = ((bf16[8,128,1024]{2,1,0:T(8,128)(2,1)}), bf16[8,128,1024]{2,1,0:T(8,128)(2,1)S(1)}, u32[]{:S(2)}, u32[]{:S(2)}) async-start(bf16[8,128,1024]{2,1,0:T(8,128)(2,1)} %bitcast.57), calls=%async_computation.1 | async-start | bytes 4194304 | tf_op jit(solution)/shard_map/all_to_all | solution.py:32
  33.5 7.8 %reshape.313 = bf16[1024,2048]{1,0:T(8,128)(2,1)} reshape(bf16[1024,4,4,128]{3,2,1,0:T(4,128)(2,1)} %param.12) | data formatting | bytes 8388608 | tf_op jit(solution)/shard_map/reshape | solution.py:35
  41.9 2.0 %copy.20 = bf16[1,512,512]{1,2,0:T(8,128)(2,1)} copy(bf16[1,512,512]{2,1,0:T(8,128)(2,1)} %param.10) | data formatting | bytes 1048576 | tf_op jit(solution)/shard_map/reshape.9
  44.0 2.0 %reshape.316 = bf16[512,4,128]{2,1,0:T(4,128)(2,1)} reshape(bf16[1,512,512]{2,1,0:T(8,128)(2,1)} %param.9) | data formatting | bytes 1048576 | tf_op jit(solution)/shard_map/reshape.6
  45.9 36.4 %all-to-all-done.1 = bf16[8,128,1024]{2,1,0:T(8,128)(2,1)S(1)} async-done(((bf16[8,128,1024]{2,1,0:T(8,128)(2,1)}), bf16[8,128,1024]{2,1,0:T(8,128)(2,1)S(1)}, u32[]{:S(2)}, u32[]{:S(2)}) %all-to-all-start.1) | async-done | bytes 2097184 | tf_op jit(solution)/shard_map/all_to_all | solution.py:32
  82.4 2.8 %gather_fusion.1 = bf16[512,1024]{1,0:T(8,128)(2,1)} fusion(bf16[1024,1024]{1,0:T(8,128)(2,1)S(1)} %bitcast.56, s32[1024]{0:T(1024)S(1)} %pad_clamp_fusion), kind=kCustom, calls=%fused_computation.1 | custom fusion | bytes 2099200 | tf_op jit(solution)/shard_map/gather | solution.py:33
  85.2 6.6 %multiply_convert_fusion = bf16[512,2048]{1,0:T(8,128)(2,1)} fusion(bf16[512,1024]{1,0:T(8,128)(2,1)} %gather_fusion.1, bf16[1024,2048]{1,0:T(8,128)(2,1)} %reshape.313), kind=kOutput, calls=%fused_computation.4 | convolution fusion | flops 2152726528 | bytes 7340032 | tf_op jit(solution)/shard_map/dot_general | solution.py:34
  91.8 3.2 %reshape.314 = bf16[1,512,4,4,128]{4,3,2,1,0:T(4,128)(2,1)S(1)} reshape(bf16[512,2048]{1,0:T(8,128)(2,1)} %multiply_convert_fusion) | data formatting | bytes 4194304 | tf_op jit(solution)/shard_map/reshape | solution.py:38
  95.0 4.5 %fusion.24 = (bf16[1,512,4,1,128]{4,3,2,1,0:T(2,128)(2,1)}, bf16[1,512,4,1,128]{4,3,2,1,0:T(2,128)(2,1)}, bf16[1,512,4,1,128]{4,3,2,1,0:T(2,128)(2,1)}, bf16[1,512,4,1,128]{4,3,2,1,0:T(2,128)(2,1)}) fusion(bf16[1,512,4,4,128]{4,3,2,1,0:T(4,128)(2,1)S(1)} %reshape.314), kind=kLoop, calls=%fused_computation.61 | loop fusion | bytes 4194304 | tf_op jit(solution)/shard_map/slice | solution.py:42
  99.5 2.3 %copy.23 = bf16[1,512,4,1,128]{1,4,2,3,0:T(8,128)(2,1)S(1)} copy(bf16[1,512,4,1,128]{4,3,2,1,0:T(2,128)(2,1)} %get-tuple-element.12) | data formatting | bytes 1048576
  101.9 1.9 %multiply_reduce_fusion.1 = f32[512,4]{0,1:T(4,128)S(1)} fusion(bf16[1,512,4,1,128]{4,3,2,1,0:T(2,128)(2,1)} %get-tuple-element.10, bf16[1,512,4,1,128]{4,3,2,1,0:T(2,128)(2,1)} %get-tuple-element.11), kind=kLoop, calls=%fused_computation.17 | loop fusion | flops 1046528 | bytes 1056768 | tf_op jit(solution)/shard_map/reduce_sum | solution.py:53
  103.8 4.7 %multiply_reduce_fusion = (f32[512,4]{0,1:T(4,128)S(1)}, f32[1,512,4,128]{1,3,2,0:T(8,128)}) fusion(bf16[1,512,4,1,128]{1,4,2,3,0:T(8,128)(2,1)S(1)} %copy.23, f32[512,4]{0,1:T(4,128)S(1)} %fusion.14, bf16[512,4,128]{0,2,1:T(8,128)(2,1)} %bitcast.58, f32[]{:T(128)} %bitcast.13, pred[512]{0:T(512)(128)(4,1)S(1)} %iota_compare_fusion.2, ...), kind=kOutput, calls=%fused_computation.16 | convolution fusion | flops 546568192 | bytes 3162628 | tf_op jit(solution)/shard_map/uhcp,uphd->uchd/dot_general | solution.py:50
  108.5 2.3 %copy.24 = bf16[1,512,4,1,128]{1,4,2,3,0:T(8,128)(2,1)} copy(bf16[1,512,4,1,128]{4,3,2,1,0:T(2,128)(2,1)S(1)} %copy-done.1) | data formatting | bytes 1048576
  110.8 1.5 %fusion.5 = bf16[1,512,4,128]{1,3,2,0:T(8,128)(2,1)S(1)} fusion(f32[1,512,4,128]{1,3,2,0:T(8,128)} %get-tuple-element.16, bf16[1,512,4,1,128]{1,4,2,3,0:T(8,128)(2,1)} %copy.24, f32[512,4]{0,1:T(4,128)S(1)} %add_rsqrt_fusion), kind=kLoop, calls=%fused_computation.14 | loop fusion | flops 1048576 | bytes 2105344 | tf_op jit(solution)/shard_map/convert_element_type | solution.py:57
  112.4 2.9 %convolution_convert_fusion = bf16[512,1024]{1,0:T(8,128)(2,1)} fusion(bf16[512,512]{0,1:T(8,128)(2,1)S(1)} %bitcast.59, bf16[512,1024]{1,0:T(8,128)(2,1)} %bitcast.67), kind=kOutput, calls=%fused_computation.5 | convolution fusion | flops 537395200 | bytes 2621440 | tf_op jit(solution)/shard_map/dot_general | solution.py:60
  115.3 19.4 %reduce-scatter.2.cloned.1.call-done = bf16[512,512]{1,0:T(8,128)(2,1)} async-done(((bf16[512,1024]{1,0:T(8,128)(2,1)}), bf16[512,512]{1,0:T(8,128)(2,1)}) %reduce-scatter.2.cloned.1.call-update) | async-done | bytes 524304 | tf_op jit(solution)/shard_map/reduce_scatter | solution.py:67
  134.8 1.3 fusion.3
  136.1 4.9 %all-reduce = (f32[512]{0:T(512)S(1)}, f32[512]{0:T(512)S(1)}) all-reduce(f32[512]{0:T(512)S(1)} %get-tuple-element.6, f32[512]{0:T(512)S(1)} %get-tuple-element.5), channel_id=1, replica_groups=mesh['grp'=2,'user'=8,'head'=2] {'head'}, use_global_device_ids=true, to_apply=%region_10.11 | all-reduce | flops 1024 | bytes 8192 | tf_op jit(solution)/shard_map/psum | solution.py:75
  (21 shorter events, 1.8 us)
Async XLA Ops:
  6.5 17.9 %copy-start = (bf16[512,1024]{1,0:T(8,128)(2,1)S(1)}, bf16[512,1024]{1,0:T(8,128)(2,1)}, u32[]{:S(2)}) copy-start(bf16[512,1024]{1,0:T(8,128)(2,1)} %param.11) | copy-start | bytes 3145732
  29.8 52.6 %all-to-all-start.1 = ((bf16[8,128,1024]{2,1,0:T(8,128)(2,1)}), bf16[8,128,1024]{2,1,0:T(8,128)(2,1)S(1)}, u32[]{:S(2)}, u32[]{:S(2)}) async-start(bf16[8,128,1024]{2,1,0:T(8,128)(2,1)} %bitcast.57), calls=%async_computation.1 | async-start | bytes 4194304 | tf_op jit(solution)/shard_map/all_to_all | solution.py:32
  33.4 101.4 %reduce-scatter.2.cloned.1.call-start = ((), (), s32[]{:S(2)}) async-start(), calls=%async_computation.3 | async-start | bytes 1572864 | tf_op jit(solution)/shard_map/reduce_scatter | solution.py:67
  103.8 4.8 %copy-start.1 = (bf16[1,512,4,1,128]{4,3,2,1,0:T(2,128)(2,1)S(1)}, bf16[1,512,4,1,128]{4,3,2,1,0:T(2,128)(2,1)}, u32[]{:S(2)}) copy-start(bf16[1,512,4,1,128]{4,3,2,1,0:T(2,128)(2,1)} %get-tuple-element.9) | copy-start | bytes 1572868
  108.5 26.2 %copy-start.2 = (bf16[512,1024]{1,0:T(8,128)(2,1)S(1)}, bf16[512,1024]{1,0:T(8,128)(2,1)}, u32[]{:S(2)}) copy-start(bf16[512,1024]{1,0:T(8,128)(2,1)} %gather_fusion.1) | copy-start | bytes 3145732
Sparse Core Ops, SparseCore 0:
  115.4 19.2 reduce-scatter.1
where the time goes:
time: 149 us; the launch traced here: 148 us
  waiting for transfers between devices  55.9 us (38%)
  local copies, waits for them, and re-layouts  35 us (23%)
  blocking collectives  16.7 us (11%)
  matrix products  14.3 us (10%)
  between operations  14.1 us (9%)
  other arithmetic  8.84 us (6%)
  starting transfers between devices  3.64 us (2%)
    all_to_all x1, waiting for transfers between devices, body(): lax.all_to_all(looked_up, 'user', split_axis=0, concat_axis=0, tiled=True)  36.4 us
    reduce_scatter x1, waiting for transfers between devices, body(): lax.psum_scatter(partial_value.astype(jnp.bfloat16), 'head', scatter_dime...  19.4 us
    all_to_all x1, blocking collectives, body(): lax.all_to_all(requests.reshape(shard_count, capacity), 'user', split_axi...  11.7 us
    reshape x1, local copies, waits for them, and re-layouts, body(): w_qkvu.reshape(model_width, -1)  7.8 us
    dot_general x1, matrix products, body(): jnp.dot(embedded, w_qkvu.reshape(model_width, -1), preferred_element_type...  6.63 us
    gather x1, local copies, waits for them, and re-layouts, body(): item_table[safe_rows].reshape(shard_count, capacity, model_width)  5.37 us
    psum x1, blocking collectives, body(): square_total, inner_total = lax.psum((square_part, inner_part), 'head')  4.93 us
    dot_general x1, matrix products, body(): jnp.einsum('uhcp,uphd->uchd', weights, cached_values, preferred_element_t...  4.74 us
  transfers between devices with their start and end apart: 2, of which 2 were waited for; matrix products, arithmetic and copies ran while one was open for 8% of the time, Pallas kernels for 0%

commit v1 on v0

v1 whole, which is shorter than its diff:
```python
import functools

import jax
import jax.numpy as jnp
from jax import lax
from jax.experimental import pallas as pl
from jax.experimental.pallas import tpu as pltpu
from jax.sharding import PartitionSpec as P

AXES = ("grp", "user", "head")


def silu_f32(value):
    half = 0.5 * value
    return half + half * jnp.tanh(half)


def select_kernel(base_ref, ids_ref, *refs, pieces, groups, has_prev):
    piece_refs = refs[:pieces]
    prev_refs = refs[pieces : pieces + groups] if has_prev else None
    out_refs = refs[len(refs) - groups - 1 : len(refs) - 1]
    hot_ref = refs[-1]
    rows = piece_refs[0].shape[0]
    count = ids_ref.shape[1]
    step = min(count, 128)
    for j in range(groups):
        for i in range(pieces):
            for start in range(0, count, step):
                local = ids_ref[j, start : start + step, :] - base_ref[i]
                lane = lax.broadcasted_iota(jnp.int32, (step, rows), 1)
                hot_ref[start : start + step, i * rows : (i + 1) * rows] = jnp.where(
                    lane == local, 1.0, 0.0
                ).astype(jnp.bfloat16)
        total = None
        for i in range(pieces):
            part = jnp.dot(
                hot_ref[:, i * rows : (i + 1) * rows],
                piece_refs[i][...],
                preferred_element_type=jnp.float32,
            )
            total = part if total is None else total + part
        if has_prev:
            total = total + prev_refs[j][...].astype(jnp.float32)
        out_refs[j][...] = total.astype(jnp.bfloat16)


def select_rows(bases, ids, pieces, prev=None):
    groups, count = ids.shape[0], ids.shape[1]
    rows, feats = pieces[0].shape
    vmem = pl.BlockSpec(memory_space=pltpu.VMEM)
    extra = [] if prev is None else list(prev)
    return pl.pallas_call(
        functools.partial(
            select_kernel, pieces=len(pieces), groups=groups, has_prev=prev is not None
        ),
        out_shape=[jax.ShapeDtypeStruct((count, feats), jnp.bfloat16)] * groups,
        in_specs=[pl.BlockSpec(memory_space=pltpu.SMEM)] + [vmem] * (1 + len(pieces) + len(extra)),
        out_specs=[vmem] * groups,
        scratch_shapes=[pltpu.VMEM((count, rows * len(pieces)), jnp.bfloat16)],
        cost_estimate=pl.CostEstimate(
            flops=2 * groups * count * rows * len(pieces) * feats,
            bytes_accessed=2 * rows * len(pieces) * feats,
            transcendentals=0,
        ),
        name="select_rows",
    )(bases, ids, *pieces, *extra)


def attend_kernel(int_ref, float_ref, *refs, parts, scale):
    part_refs = refs[:parts]
    w_ref, k_ref, v_ref, out_ref = refs[parts:]
    feats = part_refs[0].shape[1]
    rows = out_ref.shape[0]
    size = k_ref.shape[1]
    length = int_ref[parts]
    inverse = float_ref[0]
    position = lax.broadcasted_iota(jnp.int32, v_ref.shape, 0)
    values = jnp.where(position < length, v_ref[...].astype(jnp.float32), 0.0).astype(jnp.bfloat16)
    step = min(rows, 256)
    for start in range(0, rows, step):
        projected = None
        for i in range(parts):
            w_rows = w_ref[pl.ds(pl.multiple_of(int_ref[i] * feats, feats), feats), :]
            piece = jnp.dot(
                part_refs[i][start : start + step, :], w_rows, preferred_element_type=jnp.float32
            )
            projected = piece if projected is None else projected + piece
        activated = silu_f32(projected).astype(jnp.bfloat16)
        queries = activated[:, :size]
        own_keys = activated[:, size : 2 * size].astype(jnp.float32)
        own_values = activated[:, 2 * size : 3 * size].astype(jnp.float32)
        gates = activated[:, 3 * size :].astype(jnp.float32)
        raw = lax.dot_general(
            queries, k_ref[...], (((1,), (1,)), ((), ())), preferred_element_type=jnp.float32
        )
        weights = (silu_f32(raw * scale) * inverse).astype(jnp.bfloat16)
        attended = jnp.dot(weights, values, preferred_element_type=jnp.float32)
        own_dot = jnp.sum(queries.astype(jnp.float32) * own_keys, axis=-1, keepdims=True)
        attended = attended + (silu_f32(own_dot * scale) * inverse) * own_values
        mean_square = jnp.mean(attended * attended, axis=-1, keepdims=True)
        out_ref[start : start + step, :] = (
            attended * lax.rsqrt(mean_square + 1e-06) * gates
        ).astype(jnp.bfloat16)


def attend(ints, floats, parts, w_flat, keys, values, heads, size):
    rows, feats = parts[0].shape
    width = w_flat.shape[0]
    prefix = keys.shape[0]
    smem = pl.BlockSpec(memory_space=pltpu.SMEM)
    return pl.pallas_call(
        functools.partial(attend_kernel, parts=len(parts), scale=size ** (-0.5)),
        grid=(heads,),
        out_shape=jax.ShapeDtypeStruct((rows, heads * size), jnp.bfloat16),
        in_specs=[smem, smem]
        + [pl.BlockSpec((rows, feats), lambda j: (0, 0))] * len(parts)
        + [
            pl.BlockSpec((width, 4 * size), lambda j: (0, j)),
            pl.BlockSpec((prefix, size), lambda j: (0, j)),
            pl.BlockSpec((prefix, size), lambda j: (0, j)),
        ],
        out_specs=pl.BlockSpec((rows, size), lambda j: (0, j)),
        cost_estimate=pl.CostEstimate(
            flops=2 * rows * heads * size * (4 * width + 2 * prefix),
            bytes_accessed=2 * (w_flat.size + keys.size + values.size + 2 * rows * width),
            transcendentals=rows * heads * (4 * size + prefix),
        ),
        name="attend",
    )(ints, floats, *parts, w_flat, keys, values)


def lane_sum_row(product):
    rows, width = product.shape
    folded = product[:, :128]
    for start in range(128, width, 128):
        folded = folded + product[:, start : start + 128]
    return jnp.sum(folded.T, axis=0, keepdims=True)


def score_kernel(int_ref, *refs, parts, groups, width):
    gated_refs = refs[:groups]
    w_refs = refs[groups : 2 * groups]
    part_refs = refs[2 * groups : 2 * groups + parts]
    out_ref, sum_ref = refs[2 * groups + parts :]
    feats = part_refs[0].shape[1]
    summed = None
    for i in range(groups):
        partial = jnp.dot(
            gated_refs[i][...], w_refs[i][...], preferred_element_type=jnp.float32
        ).astype(jnp.bfloat16).astype(jnp.float32)
        summed = partial if summed is None else summed + partial
    square = lane_sum_row(summed * summed)
    for i in range(width // feats):
        sum_ref[i] = summed[:, i * feats : (i + 1) * feats]
    product = None
    for i in range(parts):
        term = sum_ref[int_ref[i]] * part_refs[i][...].astype(jnp.float32)
        product = term if product is None else product + term
    inner = lane_sum_row(product)
    out_ref[...] = inner * width ** (-0.5) * lax.rsqrt(square * (1.0 / width) + 1e-06)


def score_rows(ints, row_block, gated, w_out, parts, rows):
    groups = len(gated)
    feats = parts[0].shape[1]
    width = w_out[0].shape[1]
    depth = w_out[0].shape[0]
    block = lambda c: pl.BlockSpec((rows, c), lambda i, ints: (ints[len(parts)], 0))
    whole = lambda r, c: pl.BlockSpec((r, c), lambda i, ints: (0, 0))
    return pl.pallas_call(
        functools.partial(score_kernel, parts=len(parts), groups=groups, width=width),
        grid_spec=pltpu.PrefetchScalarGridSpec(
            num_scalar_prefetch=1,
            grid=(1,),
            in_specs=[block(depth)]
            + [whole(rows, depth)] * (groups - 1)
            + [whole(depth, width)] * groups
            + [block(feats)] * len(parts),
            out_specs=whole(1, rows),
            scratch_shapes=[pltpu.VMEM((width // feats, rows, feats), jnp.float32)],
        ),
        out_shape=jax.ShapeDtypeStruct((1, rows), jnp.float32),
        cost_estimate=pl.CostEstimate(
            flops=2 * rows * groups * depth * width,
            bytes_accessed=2 * groups * depth * width,
            transcendentals=rows,
        ),
        name="score_rows",
    )(ints, *gated, *w_out, *parts)


def body(cand_ids, prefix_len, key_cache, value_cache, item_table, w_qkvu, w_out):
    grp_size, user_size, head_size = (lax.axis_size(name) for name in AXES)
    grp, user, head = (lax.axis_index(name) for name in AXES)
    cand_count = cand_ids.shape[0] * cand_ids.shape[1]
    rows_shard, width = item_table.shape
    heads_here, size = w_qkvu.shape[1], w_qkvu.shape[3]
    prefix = key_cache.shape[1]
    columns = grp_size * head_size
    feats = width // columns

    def device(g, u, h):
        return (g * user_size + u) * head_size + h

    def move(value, target):
        pairs = [
            (device(g, u, h), device(*target(g, u, h)))
            for g in range(grp_size)
            for u in range(user_size)
            for h in range(head_size)
        ]
        return lax.ppermute(value, AXES, pairs)

    column = grp * head_size + head
    own = lax.dynamic_slice_in_dim(item_table, column * feats, feats, 1)
    ids = [cand_ids.reshape(-1)]
    for dg in range(1, grp_size):
        ids.append(move(ids[0], lambda g, u, h, dg=dg: ((g - dg) % grp_size, u, h)))
    ids = jnp.stack(ids).reshape(grp_size, cand_count, 1)
    pieces, masks = [own], [0]
    distance = user_size // 2
    while distance >= 1:
        pieces += [move(p, lambda g, u, h: (g, u ^ distance, h)) for p in pieces]
        masks += [m | distance for m in masks]
        distance //= 2
    bases = [(user ^ m) * rows_shard for m in masks]
    late = [i for i, m in enumerate(masks) if m | 1 == user_size - 1]
    early = [i for i in range(len(masks)) if i not in late]
    take = lambda values, where: [values[i] for i in where]
    chosen = None
    if early:
        chosen = select_rows(jnp.stack(take(bases, early)), ids, take(pieces, early))
    chosen = select_rows(jnp.stack(take(bases, late)), ids, take(pieces, late), chosen)

    parts, order = [chosen[0]], [column]
    for dg in range(grp_size):
        for dh in range(head_size):
            if dg == 0 and dh == 0:
                continue
            parts.append(
                move(
                    chosen[dg],
                    lambda g, u, h: ((g + dg) % grp_size, u, (h + dh) % head_size),
                )
            )
            order.append(
                ((grp - dg) % grp_size) * head_size + (head - dh) % head_size
            )

    ints = jnp.stack(order + [prefix_len[0]]).astype(jnp.int32)
    inverse = 1.0 / (prefix_len + 1).astype(jnp.float32)
    gated = attend(
        ints,
        inverse,
        parts,
        w_qkvu.reshape(width, heads_here * 4 * size),
        key_cache.reshape(prefix, heads_here * size),
        value_cache.reshape(prefix, heads_here * size),
        heads_here,
        size,
    )

    rows = cand_count // head_size
    w_here = w_out.reshape(heads_here * size, width)
    gated_parts, w_parts = [gated], [w_here]
    for dh in range(1, head_size):
        target = lambda g, u, h: (g, u, (h + dh) % head_size)
        block = lax.dynamic_slice_in_dim(gated, ((head + dh) % head_size) * rows, rows, 0)
        gated_parts.append(move(block, target))
        w_parts.append(move(w_here, target))
    score_ints = jnp.stack(order + [head]).astype(jnp.int32)
    mine = score_rows(score_ints, head, gated_parts, w_parts, parts, rows)
    blocks = [mine]
    for dh in range(1, head_size):
        blocks.append(move(mine, lambda g, u, h: (g, u, (h - dh) % head_size)))
    ordered = []
    for b in range(head_size):
        value = blocks[0]
        for dh in range(1, head_size):
            value = jnp.where((head + dh) % head_size == b, blocks[dh], value)
        ordered.append(value)
    return jnp.concatenate(ordered, axis=1).reshape(cand_ids.shape)


def solution(mesh):
    in_specs = (
        P(("grp", "user"), None),
        P(("grp", "user")),
        P(("grp", "user"), None, "head"),
        P(("grp", "user"), None, "head"),
        P("user", None),
        P(None, "head", None, None),
        P("head", None, None),
    )
    out_specs = P(("grp", "user"), None)
    return jax.shard_map(body, mesh=mesh, in_specs=in_specs, out_specs=out_specs, check_vma=False)
```

time: 149 us -> 86.9 us (0.58)
  waiting for transfers between devices: 55.9 us -> 31.9 us
  local copies, waits for them, and re-layouts: 35 us -> 15.1 us
  Pallas kernels: 0 us -> 19.7 us
  blocking collectives: 16.7 us -> 0 us
  matrix products: 14.3 us -> 0 us
  between operations: 14.1 us -> 0.79 us
  starting transfers between devices: 3.64 us -> 16.5 us
  other arithmetic: 8.84 us -> 2.51 us
    all_to_all x1 -> x0, waiting for transfers between devices: 36.4 us -> none  [body(): lax.all_to_all(looked_up, 'user', split_axis=0, concat_axis=0, tiled=True)]
    ppermute x0 -> x14, waiting for transfers between devices: none -> 31.9 us  [move(): return lax.ppermute(value, AXES, pairs)]
    pallas_call x0 -> x4, Pallas kernels: none -> 19.7 us  [the longest x1 8.56 us: attend(): pl.pallas_call(functools.partial(attend_kernel, parts=len(parts), scale=s...]
    reduce_scatter x1 -> x0, waiting for transfers between devices: 19.4 us -> none  [body(): lax.psum_scatter(partial_value.astype(jnp.bfloat16), 'head', scatter_dime...]
    ppermute x0 -> x14, starting transfers between devices: none -> 16.5 us  [move(): return lax.ppermute(value, AXES, pairs)]
    dot_general x3 -> x0, matrix products: 14.3 us -> none  [the longest x1 6.63 us: body(): jnp.dot(embedded, w_qkvu.reshape(model_width, -1), preferred_element_type...]
    all_to_all x1 -> x0, blocking collectives: 11.7 us -> none  [body(): lax.all_to_all(requests.reshape(shard_count, capacity), 'user', split_axi...]
    gather x2 -> x0, local copies, waits for them, and re-layouts: 8.16 us -> none  [the longest x1 5.37 us: body(): item_table[safe_rows].reshape(shard_count, capacity, model_width)]
  transfers between devices with their start and end apart: 2 -> 14, of which waited for: 2 -> 7; matrix products, arithmetic and copies ran while one was open for 8% -> 15% of each run, Pallas kernels for 0% -> 18%
where the time goes in v1:
time: 86.9 us; the launch traced here: 86.5 us
  waiting for transfers between devices  31.9 us (37%)
  Pallas kernels  19.7 us (23%)
  starting transfers between devices  16.5 us (19%)
  local copies, waits for them, and re-layouts  15.1 us (17%)
  other arithmetic  2.51 us (3%)
    ppermute x14, waiting for transfers between devices, move(): return lax.ppermute(value, AXES, pairs)  31.9 us
    ppermute x14, starting transfers between devices, move(): return lax.ppermute(value, AXES, pairs)  16.5 us
    pallas_call x1, Pallas kernels, attend(): pl.pallas_call(functools.partial(attend_kernel, parts=len(parts), scale=s...  8.56 us
    reshape x1, local copies, waits for them, and re-layouts, body(): w_qkvu.reshape(width, heads_here * 4 * size)  7.8 us
    pallas_call x2, Pallas kernels, select_rows(): pl.pallas_call(functools.partial(select_kernel, pieces=len(pieces), group...  7.19 us
    pallas_call x1, Pallas kernels, score_rows(): pl.pallas_call(functools.partial(score_kernel, parts=len(parts), groups=g...  3.96 us
    unnamed x22, local copies, waits for them, and re-layouts  3.31 us
  transfers between devices with their start and end apart: 14, of which 7 were waited for; matrix products, arithmetic and copies ran while one was open for 15% of the time, Pallas kernels for 18%

profile of v1, /device:TPU:0, one launch (start us, length us, event | category | flops | bytes accessed | tf_op | source)
XLA Modules:
  0.0 86.5 jit_solution(9497108703560426308)
XLA Ops:
  0.0 1.2 %copy-done = bf16[512,1024]{1,0:T(8,128)(2,1)S(1)} copy-done((bf16[512,1024]{1,0:T(8,128)(2,1)S(1)}, bf16[512,1024]{1,0:T(8,128)(2,1)}, u32[]{:S(2)}) %copy-start) | copy-done | bytes 1048600
  1.3 4.1 %collective-permute-start.1 = (bf16[512,256]{1,0:T(8,128)(2,1)S(1)}, bf16[512,256]{1,0:T(8,128)(2,1)S(1)}, u32[]{:S(2)}, u32[]{:S(2)}) collective-permute-start(bf16[512,256]{1,0:T(8,128)(2,1)S(1)} %constant_dynamic-slice_fusion.1.refs_0_), channel_id=1, source_target_pairs={{0,8},{1,9},{2,10},{3,11},{4,12},{5,13},{6,14},{7,15},{8,0},{9,1},... | collective-permute-start | bytes 786440 | tf_op jit(solution)/shard_map/ppermute | solution.py:212
  5.4 1.6 %collective-permute-start.4 = (bf16[512,256]{1,0:T(8,128)(2,1)S(1)}, bf16[512,256]{1,0:T(8,128)(2,1)S(1)}, u32[]{:S(2)}, u32[]{:S(2)}) collective-permute-start(bf16[512,256]{1,0:T(8,128)(2,1)S(1)} %constant_dynamic-slice_fusion.1.refs_0_), channel_id=1, source_target_pairs={{0,4},{1,5},{2,6},{3,7},{4,0},{5,1},{6,2},{7,3},{8,12},{9,13},{10,... | collective-permute-start | bytes 786440 | tf_op jit(solution)/shard_map/ppermute | solution.py:212
  7.0 10.4 %collective-permute-done.1.refs_1_ = bf16[512,256]{1,0:T(8,128)(2,1)S(1)} collective-permute-done((bf16[512,256]{1,0:T(8,128)(2,1)S(1)}, bf16[512,256]{1,0:T(8,128)(2,1)S(1)}, u32[]{:S(2)}, u32[]{:S(2)}) %collective-permute-start.1) | collective-permute-done | bytes 262176 | tf_op jit(solution)/shard_map/ppermute | solution.py:212
  18.6 1.5 %collective-permute-start = (s32[512]{0:T(512)}, s32[512]{0:T(512)S(1)}, u32[]{:S(2)}, u32[]{:S(2)}) collective-permute-start(s32[512]{0:T(512)} %bitcast.22), channel_id=1, source_target_pairs={{0,16},{1,17},{2,18},{3,19},{4,20},{5,21},{6,22},{7,23},{8,24},{9,... | collective-permute-start | bytes 6152 | tf_op jit(solution)/shard_map/ppermute | solution.py:212
  21.4 1.0 %collective-permute-done = s32[512]{0:T(512)S(1)} collective-permute-done((s32[512]{0:T(512)}, s32[512]{0:T(512)S(1)}, u32[]{:S(2)}, u32[]{:S(2)}) %collective-permute-start) | collective-permute-done | bytes 2080 | tf_op jit(solution)/shard_map/ppermute | solution.py:212
  22.4 1.5 %collective-permute-start.12 = (bf16[512,1024]{1,0:T(8,128)(2,1)}, bf16[512,1024]{1,0:T(8,128)(2,1)S(1)}, u32[]{:S(2)}, u32[]{:S(2)}) collective-permute-start(bf16[512,1024]{1,0:T(8,128)(2,1)} %bitcast.20), channel_id=1, source_target_pairs={{0,1},{1,0},{2,3},{3,2},{4,5},{5,4},{6,7},{7,6},{8,9},{9,8},{10,11... | collective-permute-start | bytes 3145736 | tf_op jit(solution)/shard_map/ppermute | solution.py:212
  23.9 0.9 %collective-permute-done.2.refs_0_ = bf16[512,256]{1,0:T(8,128)(2,1)S(1)} collective-permute-done((bf16[512,256]{1,0:T(8,128)(2,1)S(1)}, bf16[512,256]{1,0:T(8,128)(2,1)S(1)}, u32[]{:S(2)}, u32[]{:S(2)}) %collective-permute-start.2) | collective-permute-done | bytes 262176 | tf_op jit(solution)/shard_map/ppermute | solution.py:212
  25.5 1.0 %copy.9.ids_ref = s32[2,512,1]{2,1,0:T(8,128)} copy(s32[2,512,1]{1,0,2:T(2,128)S(1)} %add_bitcast_fusion) | data formatting | bytes 8192 | tf_op jit(solution)/shard_map/reshape | solution.py:219
  27.3 4.2 %select_rows.2 = (bf16[512,256]{1,0:T(8,128)(2,1)}, bf16[512,256]{1,0:T(8,128)(2,1)}) custom-call(s32[6]{0:T(128)} %stack.79.base_ref, s32[2,512,1]{2,1,0:T(8,128)} %copy.9.ids_ref, bf16[512,256]{1,0:T(8,128)(2,1)} %copy-done.6, bf16[512,256]{1,0:T(8,128)(2,1)} %copy-done.8, bf16[512,256]{1,0:T(8,128)(2,1)} %copy-done.9, bf16[512,256]{1,0:T(8,128)(2,1)} %copy-done.10, ...), custom_call_target="tpu_custom_call" | custom-call | flops 1610612736 | bytes 1572864 | tf_op jit(solution)/shard_map/select_rows/pallas_call | solution.py:52
  31.5 3.0 %select_rows.3 = (bf16[512,256]{1,0:T(8,128)(2,1)}, bf16[512,256]{1,0:T(8,128)(2,1)}) custom-call(s32[2]{0:T(128)} %pad_add_fusion.base_ref, s32[2,512,1]{2,1,0:T(8,128)} %copy.9.ids_ref, bf16[512,256]{1,0:T(8,128)(2,1)} %copy-done.7, bf16[512,256]{1,0:T(8,128)(2,1)} %collective-permute-done.3.refs_1_, bf16[512,256]{1,0:T(8,128)(2,1)} %get-tuple-element.9.refs_2_, ...), custom_call_target="tpu_custom_call" | custom-call | flops 536870912 | bytes 524288 | tf_op jit(solution)/shard_map/select_rows/pallas_call | solution.py:52
  34.5 1.3 %collective-permute-start.8 = (bf16[512,256]{1,0:T(8,128)(2,1)}, bf16[512,256]{1,0:T(8,128)(2,1)S(1)}, u32[]{:S(2)}, u32[]{:S(2)}) collective-permute-start(bf16[512,256]{1,0:T(8,128)(2,1)} %get-tuple-element.11.refs_0_.refs_4_), channel_id=1, source_target_pairs={{0,1},{1,0},{2,3},{3,2},{4,5},{5,4},{6,7},{7,6},{8,9},{9,8},{10,11... | collective-permute-start | bytes 786440 | tf_op jit(solution)/shard_map/ppermute | solution.py:212
  35.8 1.5 %collective-permute-start.9 = (bf16[512,256]{1,0:T(8,128)(2,1)}, bf16[512,256]{1,0:T(8,128)(2,1)S(1)}, u32[]{:S(2)}, u32[]{:S(2)}) collective-permute-start(bf16[512,256]{1,0:T(8,128)(2,1)} %get-tuple-element.12), channel_id=1, source_target_pairs={{0,16},{1,17},{2,18},{3,19},{4,20},{5,21},{6,22},{7,23},{8,24},{9,... | collective-permute-start | bytes 786440 | tf_op jit(solution)/shard_map/ppermute | solution.py:212
  38.7 7.8 %reshape.20.refs_4_ = bf16[1024,2048]{1,0:T(8,128)(2,1)} reshape(bf16[1024,4,4,128]{3,2,1,0:T(4,128)(2,1)} %param.12) | data formatting | bytes 8388608 | tf_op jit(solution)/shard_map/reshape | solution.py:256
  47.1 7.2 %collective-permute-done.8.refs_1_.refs_5_ = bf16[512,256]{1,0:T(8,128)(2,1)S(1)} collective-permute-done((bf16[512,256]{1,0:T(8,128)(2,1)}, bf16[512,256]{1,0:T(8,128)(2,1)S(1)}, u32[]{:S(2)}, u32[]{:S(2)}) %collective-permute-start.8) | collective-permute-done | bytes 262176 | tf_op jit(solution)/shard_map/ppermute | solution.py:212
  54.3 5.2 %collective-permute-done.10.refs_3_.refs_7_ = bf16[512,256]{1,0:T(8,128)(2,1)S(1)} collective-permute-done((bf16[512,256]{1,0:T(8,128)(2,1)}, bf16[512,256]{1,0:T(8,128)(2,1)S(1)}, u32[]{:S(2)}, u32[]{:S(2)}) %collective-permute-start.10) | collective-permute-done | bytes 262176 | tf_op jit(solution)/shard_map/ppermute | solution.py:212
  59.5 0.7 copy-done.4
  60.2 8.6 %attend.1.refs_0_ = bf16[512,512]{1,0:T(8,128)(2,1)} custom-call(s32[5]{0:T(128)} %stack.67.int_ref, f32[1]{0:T(128)S(6)} %div.3.float_ref, bf16[512,256]{1,0:T(8,128)(2,1)} %get-tuple-element.11.refs_0_.refs_4_, bf16[512,256]{1,0:T(8,128)(2,1)} %copy-done.2, bf16[512,256]{1,0:T(8,128)(2,1)} %copy-done.3, bf16[512,256]{1,0:T(8,128)(2,1)} %copy-done.4, ...), custom_call_target="tpu_custom_call" | custom-call | flops 2684354560 | bytes 7340032 | tf_op jit(solution)/shard_map/attend/pallas_call | solution.py:111
  68.8 1.0 %constant_dynamic-slice_fusion = bf16[256,512]{1,0:T(8,128)(2,1)S(1)} fusion(bf16[512,512]{1,0:T(8,128)(2,1)} %attend.1.refs_0_, s32[]{:T(128)S(6)} %select_n.58), kind=kLoop, calls=%fused_computation.5 | loop fusion | bytes 524292 | tf_op jit(solution)/shard_map/dynamic_slice | solution.py:268
  69.7 1.6 %collective-permute-start.11 = (bf16[256,512]{1,0:T(8,128)(2,1)S(1)}, bf16[256,512]{1,0:T(8,128)(2,1)S(1)}, u32[]{:S(2)}, u32[]{:S(2)}) collective-permute-start(bf16[256,512]{1,0:T(8,128)(2,1)S(1)} %constant_dynamic-slice_fusion), channel_id=1, source_target_pairs={{0,1},{1,0},{2,3},{3,2},{4,5},{5,4},{6,7},{7,6},{8,9},{9,8},{10,11... | collective-permute-start | bytes 786440 | tf_op jit(solution)/shard_map/ppermute | solution.py:212
  71.9 4.8 %collective-permute-done.11.refs_1_ = bf16[256,512]{1,0:T(8,128)(2,1)S(1)} collective-permute-done((bf16[256,512]{1,0:T(8,128)(2,1)S(1)}, bf16[256,512]{1,0:T(8,128)(2,1)S(1)}, u32[]{:S(2)}, u32[]{:S(2)}) %collective-permute-start.11) | collective-permute-done | bytes 262176 | tf_op jit(solution)/shard_map/ppermute | solution.py:212
  77.4 4.0 %score_rows.1 = f32[1,256]{1,0:T(1,128)} custom-call(s32[5]{0:T(128)} %stack.66.int_ref, bf16[512,512]{1,0:T(8,128)(2,1)} %attend.1.refs_0_, bf16[256,512]{1,0:T(8,128)(2,1)} %copy-done.5, bf16[512,1024]{1,0:T(8,128)(2,1)} %bitcast.21, bf16[512,1024]{1,0:T(8,128)(2,1)} %copy-done.1, bf16[512,256]{1,0:T(8,128)(2,1)} %get-tuple-element.11.refs_0_.refs_4_, ...), custom_call_target="tpu_custom_call" | custom-call | flops 536870912 | bytes 2097152 | tf_op jit(solution)/shard_map/score_rows/pallas_call | solution.py:170
  81.4 1.5 %collective-permute-start.13 = (f32[1,256]{1,0:T(1,128)}, f32[1,256]{1,0:T(1,128)S(1)}, u32[]{:S(2)}, u32[]{:S(2)}) collective-permute-start(f32[1,256]{1,0:T(1,128)} %score_rows.1), channel_id=1, source_target_pairs={{0,1},{1,0},{2,3},{3,2},{4,5},{5,4},{6,7},{7,6},{8,9},{9,8},{10,11... | collective-permute-start | bytes 3080 | tf_op jit(solution)/shard_map/ppermute | solution.py:212
  82.9 2.3 %collective-permute-done.13 = f32[1,256]{1,0:T(1,128)S(1)} collective-permute-done((f32[1,256]{1,0:T(1,128)}, f32[1,256]{1,0:T(1,128)S(1)}, u32[]{:S(2)}, u32[]{:S(2)}) %collective-permute-start.13) | collective-permute-done | bytes 1056 | tf_op jit(solution)/shard_map/ppermute | solution.py:212
  (41 shorter events, 7.8 us)
Async XLA Ops:
  0.0 1.2 %copy-start = (bf16[512,1024]{1,0:T(8,128)(2,1)S(1)}, bf16[512,1024]{1,0:T(8,128)(2,1)}, u32[]{:S(2)}) copy-start(bf16[512,1024]{1,0:T(8,128)(2,1)} %param.11) | copy-start | bytes 3145732
  1.3 25.3 %copy-start.6 = (bf16[512,256]{1,0:T(8,128)(2,1)}, bf16[512,256]{1,0:T(8,128)(2,1)S(1)}, u32[]{:S(2)}) copy-start(bf16[512,256]{1,0:T(8,128)(2,1)S(1)} %constant_dynamic-slice_fusion.1.refs_0_) | copy-start | bytes 786436
  1.3 16.2 %collective-permute-start.1 = (bf16[512,256]{1,0:T(8,128)(2,1)S(1)}, bf16[512,256]{1,0:T(8,128)(2,1)S(1)}, u32[]{:S(2)}, u32[]{:S(2)}) collective-permute-start(bf16[512,256]{1,0:T(8,128)(2,1)S(1)} %constant_dynamic-slice_fusion.1.refs_0_), channel_id=1, source_target_pairs={{0,8},{1,9},{2,10},{3,11},{4,12},{5,13},{6,14},{7,15},{8,0},{9,1},... | collective-permute-start | bytes 786440 | tf_op jit(solution)/shard_map/ppermute | solution.py:212
  5.4 13.2 %collective-permute-start.4 = (bf16[512,256]{1,0:T(8,128)(2,1)S(1)}, bf16[512,256]{1,0:T(8,128)(2,1)S(1)}, u32[]{:S(2)}, u32[]{:S(2)}) collective-permute-start(bf16[512,256]{1,0:T(8,128)(2,1)S(1)} %constant_dynamic-slice_fusion.1.refs_0_), channel_id=1, source_target_pairs={{0,4},{1,5},{2,6},{3,7},{4,0},{5,1},{6,2},{7,3},{8,12},{9,13},{10,... | collective-permute-start | bytes 786440 | tf_op jit(solution)/shard_map/ppermute | solution.py:212
  17.4 9.2 %copy-start.8 = (bf16[512,256]{1,0:T(8,128)(2,1)}, bf16[512,256]{1,0:T(8,128)(2,1)S(1)}, u32[]{:S(2)}) copy-start(bf16[512,256]{1,0:T(8,128)(2,1)S(1)} %collective-permute-done.1.refs_1_) | copy-start | bytes 786436
  17.4 7.4 %collective-permute-start.2 = (bf16[512,256]{1,0:T(8,128)(2,1)S(1)}, bf16[512,256]{1,0:T(8,128)(2,1)S(1)}, u32[]{:S(2)}, u32[]{:S(2)}) collective-permute-start(bf16[512,256]{1,0:T(8,128)(2,1)S(1)} %collective-permute-done.1.refs_1_), channel_id=1, source_target_pairs={{0,4},{1,5},{2,6},{3,7},{4,0},{5,1},{6,2},{7,3},{8,12},{9,13},{10,... | collective-permute-start | bytes 786440 | tf_op jit(solution)/shard_map/ppermute | solution.py:212
  18.1 8.5 %collective-permute-start.5 = (bf16[512,256]{1,0:T(8,128)(2,1)S(1)}, bf16[512,256]{1,0:T(8,128)(2,1)S(1)}, u32[]{:S(2)}, u32[]{:S(2)}) collective-permute-start(bf16[512,256]{1,0:T(8,128)(2,1)S(1)} %constant_dynamic-slice_fusion.1.refs_0_), channel_id=1, source_target_pairs={{0,2},{1,3},{2,0},{3,1},{4,6},{5,7},{6,4},{7,5},{8,10},{9,11},{10,... | collective-permute-start | bytes 786440 | tf_op jit(solution)/shard_map/ppermute | solution.py:212
  18.1 8.5 %collective-permute-start.6 = (bf16[512,256]{1,0:T(8,128)(2,1)S(1)}, bf16[512,256]{1,0:T(8,128)(2,1)}, u32[]{:S(2)}, u32[]{:S(2)}) collective-permute-start(bf16[512,256]{1,0:T(8,128)(2,1)S(1)} %collective-permute-done.1.refs_1_), channel_id=1, source_target_pairs={{0,2},{1,3},{2,0},{3,1},{4,6},{5,7},{6,4},{7,5},{8,10},{9,11},{10,... | collective-permute-start | bytes 786440 | tf_op jit(solution)/shard_map/ppermute | solution.py:212
  18.6 8.1 %copy-start.9 = (bf16[512,256]{1,0:T(8,128)(2,1)}, bf16[512,256]{1,0:T(8,128)(2,1)S(1)}, u32[]{:S(2)}) copy-start(bf16[512,256]{1,0:T(8,128)(2,1)S(1)} %collective-permute-done.4.refs_2_) | copy-start | bytes 786436
  18.6 8.0 %collective-permute-start.7 = (bf16[512,256]{1,0:T(8,128)(2,1)S(1)}, bf16[512,256]{1,0:T(8,128)(2,1)}, u32[]{:S(2)}, u32[]{:S(2)}) collective-permute-start(bf16[512,256]{1,0:T(8,128)(2,1)S(1)} %collective-permute-done.4.refs_2_), channel_id=1, source_target_pairs={{0,2},{1,3},{2,0},{3,1},{4,6},{5,7},{6,4},{7,5},{8,10},{9,11},{10,... | collective-permute-start | bytes 786440 | tf_op jit(solution)/shard_map/ppermute | solution.py:212
  18.6 3.8 %collective-permute-start = (s32[512]{0:T(512)}, s32[512]{0:T(512)S(1)}, u32[]{:S(2)}, u32[]{:S(2)}) collective-permute-start(s32[512]{0:T(512)} %bitcast.22), channel_id=1, source_target_pairs={{0,16},{1,17},{2,18},{3,19},{4,20},{5,21},{6,22},{7,23},{8,24},{9,... | collective-permute-start | bytes 6152 | tf_op jit(solution)/shard_map/ppermute | solution.py:212
  22.4 49.5 %collective-permute-start.12 = (bf16[512,1024]{1,0:T(8,128)(2,1)}, bf16[512,1024]{1,0:T(8,128)(2,1)S(1)}, u32[]{:S(2)}, u32[]{:S(2)}) collective-permute-start(bf16[512,1024]{1,0:T(8,128)(2,1)} %bitcast.20), channel_id=1, source_target_pairs={{0,1},{1,0},{2,3},{3,2},{4,5},{5,4},{6,7},{7,6},{8,9},{9,8},{10,11... | collective-permute-start | bytes 3145736 | tf_op jit(solution)/shard_map/ppermute | solution.py:212
  24.8 6.7 %copy-start.7 = (bf16[512,256]{1,0:T(8,128)(2,1)}, bf16[512,256]{1,0:T(8,128)(2,1)S(1)}, u32[]{:S(2)}) copy-start(bf16[512,256]{1,0:T(8,128)(2,1)S(1)} %collective-permute-done.2.refs_0_) | copy-start | bytes 786436
  24.8 6.7 %collective-permute-start.3 = (bf16[512,256]{1,0:T(8,128)(2,1)S(1)}, bf16[512,256]{1,0:T(8,128)(2,1)}, u32[]{:S(2)}, u32[]{:S(2)}) collective-permute-start(bf16[512,256]{1,0:T(8,128)(2,1)S(1)} %collective-permute-done.2.refs_0_), channel_id=1, source_target_pairs={{0,2},{1,3},{2,0},{3,1},{4,6},{5,7},{6,4},{7,5},{8,10},{9,11},{10,... | collective-permute-start | bytes 786440 | tf_op jit(solution)/shard_map/ppermute | solution.py:212
  26.6 0.7 copy-start.10
  34.5 19.8 %collective-permute-start.8 = (bf16[512,256]{1,0:T(8,128)(2,1)}, bf16[512,256]{1,0:T(8,128)(2,1)S(1)}, u32[]{:S(2)}, u32[]{:S(2)}) collective-permute-start(bf16[512,256]{1,0:T(8,128)(2,1)} %get-tuple-element.11.refs_0_.refs_4_), channel_id=1, source_target_pairs={{0,1},{1,0},{2,3},{3,2},{4,5},{5,4},{6,7},{7,6},{8,9},{9,8},{10,11... | collective-permute-start | bytes 786440 | tf_op jit(solution)/shard_map/ppermute | solution.py:212
  35.8 18.5 %collective-permute-start.9 = (bf16[512,256]{1,0:T(8,128)(2,1)}, bf16[512,256]{1,0:T(8,128)(2,1)S(1)}, u32[]{:S(2)}, u32[]{:S(2)}) collective-permute-start(bf16[512,256]{1,0:T(8,128)(2,1)} %get-tuple-element.12), channel_id=1, source_target_pairs={{0,16},{1,17},{2,18},{3,19},{4,20},{5,21},{6,22},{7,23},{8,24},{9,... | collective-permute-start | bytes 786440 | tf_op jit(solution)/shard_map/ppermute | solution.py:212
  37.3 22.2 %collective-permute-start.10 = (bf16[512,256]{1,0:T(8,128)(2,1)}, bf16[512,256]{1,0:T(8,128)(2,1)S(1)}, u32[]{:S(2)}, u32[]{:S(2)}) collective-permute-start(bf16[512,256]{1,0:T(8,128)(2,1)} %get-tuple-element.12), channel_id=1, source_target_pairs={{0,17},{1,16},{2,19},{3,18},{4,21},{5,20},{6,23},{7,22},{8,25},{9,... | collective-permute-start | bytes 786440 | tf_op jit(solution)/shard_map/ppermute | solution.py:212
  54.3 5.2 %copy-start.2 = (bf16[512,256]{1,0:T(8,128)(2,1)}, bf16[512,256]{1,0:T(8,128)(2,1)S(1)}, u32[]{:S(2)}) copy-start(bf16[512,256]{1,0:T(8,128)(2,1)S(1)} %collective-permute-done.8.refs_1_.refs_5_) | copy-start | bytes 786436
  54.3 5.2 %copy-start.3 = (bf16[512,256]{1,0:T(8,128)(2,1)}, bf16[512,256]{1,0:T(8,128)(2,1)S(1)}, u32[]{:S(2)}) copy-start(bf16[512,256]{1,0:T(8,128)(2,1)S(1)} %collective-permute-done.9.refs_2_.refs_6_) | copy-start | bytes 786436
  59.5 0.7 copy-start.4
  69.7 7.0 %collective-permute-start.11 = (bf16[256,512]{1,0:T(8,128)(2,1)S(1)}, bf16[256,512]{1,0:T(8,128)(2,1)S(1)}, u32[]{:S(2)}, u32[]{:S(2)}) collective-permute-start(bf16[256,512]{1,0:T(8,128)(2,1)S(1)} %constant_dynamic-slice_fusion), channel_id=1, source_target_pairs={{0,1},{1,0},{2,3},{3,2},{4,5},{5,4},{6,7},{7,6},{8,9},{9,8},{10,11... | collective-permute-start | bytes 786440 | tf_op jit(solution)/shard_map/ppermute | solution.py:212
  71.9 4.8 %copy-start.1 = (bf16[512,1024]{1,0:T(8,128)(2,1)}, bf16[512,1024]{1,0:T(8,128)(2,1)S(1)}, u32[]{:S(2)}) copy-start(bf16[512,1024]{1,0:T(8,128)(2,1)S(1)} %collective-permute-done.12.refs_3_) | copy-start | bytes 3145732
  81.4 3.8 %collective-permute-start.13 = (f32[1,256]{1,0:T(1,128)}, f32[1,256]{1,0:T(1,128)S(1)}, u32[]{:S(2)}, u32[]{:S(2)}) collective-permute-start(f32[1,256]{1,0:T(1,128)} %score_rows.1), channel_id=1, source_target_pairs={{0,1},{1,0},{2,3},{3,2},{4,5},{5,4},{6,7},{7,6},{8,9},{9,8},{10,11... | collective-permute-start | bytes 3080 | tf_op jit(solution)/shard_map/ppermute | solution.py:212
  (1 other events, 0.7 us)
